TPU v7x, 32 devices: a whole 2x2x4 slice. The times are simulated.
32 devices in a mesh: tm: 8 (over z, y), coef: 4 (over x, core).
Axes of the slice: x: 2, y: 2, z: 4, core: 2. Of those that a mesh axis runs over, the one named last changes fastest.
Arguments:
- design: bfloat16 [2048, 50176], P('tm', 'coef'), may hold values from -0.0390625 to 0.0390625
- observed: float32 [2048, 128], P('tm'), may hold values from -6 to 6
- slab_counts: int32 [8], P('tm'), may hold values from 128 to 256, as said below
- gap_mask: int32 [2048], P('tm'), may hold values 0 or 1
- filter_taps: float32 [128], replicated, may hold values from -0.5 to 1.2, as said below
- kaula_diag: float32 [50176], P('coef'), may hold values from 0.1 to 1
- precond: float32 [50176], P('coef'), may hold values from 0.3 to 3
Outputs:
- solution: float32 [50176, 128], P(('coef', 'tm'))
- residual: float32 [50176, 128], P(('coef', 'tm'))
Inputs may be any that keep to these rules, and one draw needn't show every extreme that they name: `slab_counts`: every slab holds at most 256 valid epochs, and some slab holds exactly 256. filter_taps[0] lies between 1 and 1.2.
All inputs are finite; a program needn't handle non-finite values. No bound on the sum of `gap_mask` on one device may be relied on, other than what follows from the above.
Results may differ from a plain program's by a relative error of at most 0.0065.
The roundings to bfloat16 on the way count: a program that leaves them out, or rounds other values in their place, can miss the bound.
Values may be sent and summed in bfloat16 or wider, within the bound.
No kernel may reach another device: no remote copies, remote signals or barrier semaphores. Data moves between devices by JAX's collectives and lax.ppermute only.
A program may use at most 64 MiB of HBM per device.

v0:
```python
import jax
import jax.numpy as jnp
from jax import lax
from jax.sharding import PartitionSpec as P

ITERS = 2
LANES = 128
BOTH = ("tm", "coef")


def toeplitz(pattern, band_len):
    tiled = jnp.tile(pattern, band_len)[: band_len * (2 * band_len - 1)]
    return tiled.reshape(band_len, 2 * band_len - 1)[:, :band_len]


def block_pair(filter_taps):
    band_len = filter_taps.shape[0]
    spacer = jnp.zeros((band_len,), jnp.float32)
    reversed_taps = filter_taps[:0:-1]
    lower = jnp.concatenate([filter_taps[:1], spacer, reversed_taps])
    upper = jnp.concatenate([jnp.zeros((1,), jnp.float32), reversed_taps, spacer])
    return (toeplitz(lower, band_len), toeplitz(upper, band_len))


def forward(values, lower_block, upper_block):
    band_len = lower_block.shape[0]
    blocks = values.reshape(-1, band_len, values.shape[1])
    previous = jnp.concatenate([jnp.zeros_like(blocks[:1]), blocks[:-1]], 0)
    result = jnp.einsum("ij,bjr->bir", lower_block, blocks, precision=lax.Precision.HIGHEST)
    result = result + jnp.einsum(
        "ij,bjr->bir", upper_block, previous, precision=lax.Precision.HIGHEST
    )
    return result.reshape(values.shape)


def backward(values, lower_block, upper_block):
    band_len = lower_block.shape[0]
    blocks = values.reshape(-1, band_len, values.shape[1])
    following = jnp.concatenate([blocks[1:], jnp.zeros_like(blocks[:1])], 0)
    result = jnp.einsum("ji,bjr->bir", lower_block, blocks, precision=lax.Precision.HIGHEST)
    result = result + jnp.einsum(
        "ji,bjr->bir", upper_block, following, precision=lax.Precision.HIGHEST
    )
    return result.reshape(values.shape)


def shards(design, observed, slab_counts, gap_mask, filter_taps, kaula_diag, precond):
    epoch_rows, coef_rows = design.shape
    slabs = lax.axis_size("tm")
    owned_rows = coef_rows // slabs
    owner_index = lax.axis_index("tm")
    tile = LANES if coef_rows % LANES == 0 else owned_rows
    tiles = coef_rows // tile
    width = max(
        (-(-(slab + 1) * owned_rows // tile) - slab * owned_rows // tile for slab in range(slabs))
    )
    first_tiles = [min(slab * owned_rows // tile, tiles - width) for slab in range(slabs)]
    window = width * tile
    begins = [first * tile for first in first_tiles]
    begin = jnp.array(begins, jnp.int32)[owner_index]
    offset = owner_index * owned_rows - begin
    pieces = jnp.stack([design[:, start : start + window] for start in begins])
    columns = lax.all_to_all(pieces, "tm", 0, 0).reshape(slabs * epoch_rows, window)
    position = jnp.arange(epoch_rows, dtype=jnp.int32)
    own_weight = ((gap_mask == 1) & (position < slab_counts[0])).astype(jnp.float32)
    packed = jnp.concatenate(
        [observed, jnp.broadcast_to(own_weight[:, None], (epoch_rows, LANES))], 1
    )
    packed = lax.all_gather(packed, "tm", axis=0, tiled=True)
    observed_all = packed[:, : observed.shape[1]]
    weight = packed[:, observed.shape[1] : observed.shape[1] + 1]
    lower_block, upper_block = block_pair(filter_taps)

    def weighted(values):
        inner = forward(weight * values, lower_block, upper_block)
        return (weight * backward(inner, lower_block, upper_block)).astype(jnp.bfloat16)

    def transposed(filtered):
        return lax.dot_general(
            columns, filtered, (((0,), (0,)), ((), ())), preferred_element_type=jnp.float32
        )

    def reduced(vector, rows):
        product = jnp.dot(columns, vector.astype(jnp.bfloat16), preferred_element_type=jnp.float32)
        extra = jnp.stack(rows + [jnp.zeros_like(rows[0])] * (8 - len(rows)))
        total = lax.psum(jnp.concatenate([product, extra]), BOTH)
        return (total[: product.shape[0]], [total[product.shape[0] + i] for i in range(len(rows))])

    local = jnp.arange(window, dtype=jnp.int32)
    owned = (local >= offset) & (local < offset + owned_rows)

    def window_of(values):
        cut = lax.dynamic_slice_in_dim(values, begin, window, 0)
        return jnp.where(owned, cut, 0.0)[:, None]

    kaula_col = window_of(kaula_diag)
    precond_col = window_of(precond)
    residual = transposed(weighted(observed_all))
    solution = jnp.zeros_like(residual)
    direction = None
    for iteration in range(ITERS):
        scaled = precond_col * residual
        rows = [jnp.sum(residual * scaled, 0), jnp.sum(kaula_col * scaled * scaled, 0)]
        if iteration:
            rows.append(jnp.sum(kaula_col * scaled * direction, 0))
        product, sums = reduced(scaled, rows)
        if iteration:
            ratio = sums[0] / norm_now
            direction = scaled + ratio * direction
            slab_values = product + ratio * slab_values
            ridge = sums[1] + 2.0 * ratio * sums[2] + ratio * ratio * ridge
        else:
            direction, slab_values, ridge = (scaled, product, sums[1])
        norm_now = sums[0]
        filtered = weighted(slab_values)
        curvature = jnp.sum(slab_values * filtered.astype(jnp.float32), 0) + ridge
        image = transposed(filtered) + kaula_col * direction
        step_len = norm_now / curvature
        solution = solution + step_len * direction
        residual = residual - step_len * image
    return tuple(
        (lax.dynamic_slice_in_dim(values, offset, owned_rows, 0) for values in (solution, residual))
    )


def solution(mesh):
    placed = (P("tm", "coef"), P("tm", None), P("tm"), P("tm"), P(), P("coef"), P("coef"))
    return jax.shard_map(
        shards,
        mesh=mesh,
        in_specs=placed,
        out_specs=(P(("coef", "tm"), None), P(("coef", "tm"), None)),
        check_vma=False,
    )
```

profile of v0, /device:TPU:0, one launch (start us, length us, event | category | flops | bytes accessed | tf_op | source)
XLA Modules:
  0.0 519.3 jit_solution(8027475732928325640)
XLA Ops:
  7.2 2.3 bitcast_dynamic-update-slice_fusion.7
  9.5 2.3 bitcast_dynamic-update-slice_fusion.6
  11.7 2.2 bitcast_dynamic-update-slice_fusion.5
  13.9 2.1 bitcast_dynamic-update-slice_fusion.4
  16.1 1.0 bitcast_dynamic-update-slice_fusion.3
  17.0 1.0 bitcast_dynamic-update-slice_fusion.2
  18.0 1.0 bitcast_dynamic-update-slice_fusion.1
  19.0 1.0 bitcast_dynamic-update-slice_fusion
  20.1 7.5 %all-to-all-start = ((bf16[8,256,1664]{2,1,0:T(8,128)(2,1)}), bf16[8,256,1664]{2,1,0:T(8,128)(2,1)}, u32[]{:S(2)}, u32[]{:S(2)}) async-start(bf16[8,256,1664]{2,1,0:T(8,128)(2,1)} %bitcast_dynamic-update-slice_fusion), calls=%async_computation | async-start | bytes 13631488 | tf_op jit(solution)/shard_map/all_to_all | solution.py:63
  28.3 0.7 pad_maximum_fusion
  29.1 0.6 dynamic_slice.15
  32.1 0.3 reshape.59
  32.5 0.3 reshape.60
  33.5 0.8 dynamic-slice_select_fusion
  34.3 0.8 dynamic-slice_select_fusion.1
  35.1 140.5 %all-gather.2.cloned.1.call-done = f32[2048,256]{1,0:T(8,128)} async-done(((f32[256,256]{1,0:T(8,128)}), f32[2048,256]{1,0:T(8,128)}) %all-gather.2.cloned.1.call-update) | async-done | bytes 2097168 | tf_op jit(solution)/shard_map/all_gather | solution.py:69
  175.5 1.6 slice_reduce_fusion
  177.1 1.6 slice_multiply_fusion
  178.8 1.8 fusion.29
  180.6 1.7 fusion.4
  182.3 1.1 fusion.26
  183.4 1.1 fusion.6
  184.5 17.8 %all-to-all-done = bf16[8,256,1664]{2,1,0:T(8,128)(2,1)} async-done(((bf16[8,256,1664]{2,1,0:T(8,128)(2,1)}), bf16[8,256,1664]{2,1,0:T(8,128)(2,1)}, u32[]{:S(2)}, u32[]{:S(2)}) %all-to-all-start) | async-done | bytes 6815776 | tf_op jit(solution)/shard_map/all_to_all | solution.py:63
  202.3 5.3 %fusion.15 = (f32[128]{0:T(128)S(1)}, f32[128]{0:T(128)S(1)}, f32[1664,128]{1,0:T(8,128)S(1)}) fusion(f32[1664]{0:T(1024)S(1)} %dynamic-slice_select_fusion, f32[1664]{0:T(1024)S(1)} %dynamic-slice_select_fusion.1, bf16[2048,1664]{1,0:T(8,128)(2,1)} %bitcast.8, bf16[2048,128]{1,0:T(8,128)(2,1)S(1)} %bitcast.152), kind=kOutput, calls=%fused_computation.38 | convolution fusion | flops 873692928 | bytes 8206336 | tf_op jit(solution)/shard_map/dot_general | solution.py:79
  207.6 5.3 %fusion.20 = f32[2048,128]{1,0:T(8,128)S(1)} fusion(bf16[2048,1664]{1,0:T(8,128)(2,1)} %bitcast.8, f32[1664,128]{1,0:T(8,128)S(1)} %get-tuple-element.13, f32[1664]{0:T(1024)S(1)} %dynamic-slice_select_fusion.1), kind=kOutput, calls=%fused_computation.57 | convolution fusion | flops 872841216 | bytes 8722944 | tf_op jit(solution)/shard_map/dot_general | solution.py:84
  212.9 2.3 concatenate.42
  215.2 0.2 all-reduce.11.cloned.1.call-start
  215.4 129.3 %all-reduce.9.cloned.1.call-done = f32[2056,128]{1,0:T(8,128)} async-done(((f32[2056,128]{1,0:T(8,128)}), f32[2056,128]{1,0:T(8,128)}) %all-reduce.9.cloned.1.call-update) | async-done | bytes 1052688 | tf_op jit(solution)/shard_map/psum | solution.py:86
  344.7 1.6 slice_multiply_fusion.1
  346.4 1.8 fusion.28
  348.2 1.7 fusion.3
  349.9 1.1 fusion.25
  351.0 1.2 fusion.10
  352.2 0.4 multiply_reduce_fusion.1
  352.5 5.4 %fusion.17 = (f32[128]{0:T(128)S(1)}, f32[128]{0:T(128)S(1)}, f32[128]{0:T(128)S(1)}, f32[1664,128]{1,0:T(8,128)S(1)}) fusion(f32[1664,128]{1,0:T(8,128)S(1)} %get-tuple-element.13, f32[1664]{0:T(1024)S(1)} %dynamic-slice_select_fusion, f32[1664]{0:T(1024)S(1)} %dynamic-slice_select_fusion.1, bf16[2048,1664]{1,0:T(8,128)(2,1)} %bitcast.8, ...), kind=kOutput, calls=%fused_computation.40 | convolution fusion | flops 875183744 | bytes 9059328 | tf_op jit(solution)/shard_map/dot_general | solution.py:79
  358.0 5.1 fusion.21
  363.0 2.5 concatenate.45
  365.6 130.8 %all-reduce.11.cloned.1.call-done = f32[2056,128]{1,0:T(8,128)} async-done(((f32[2056,128]{1,0:T(8,128)}), f32[2056,128]{1,0:T(8,128)}) %all-reduce.11.cloned.1.call-update) | async-done | bytes 1052688 | tf_op jit(solution)/shard_map/psum | solution.py:86
  496.4 0.7 slice_divide_fusion
  497.1 1.4 multiply_add_fusion
  498.6 1.6 broadcast_multiply_fusion
  500.2 1.8 fusion.27
  502.0 1.7 fusion.2
  503.7 1.1 fusion.24
  504.8 1.2 fusion.9
  506.0 4.9 fusion.37
  511.0 0.4 multiply_reduce_fusion
  511.3 1.5 dynamic-slice_subtract_fusion
  (39 shorter events, 1.0 us)
Async XLA Ops:
  7.2 8.9 %copy-start.1 = (bf16[256,12544]{1,0:T(8,128)(2,1)S(1)}, bf16[256,12544]{1,0:T(8,128)(2,1)}, u32[]{:S(2)}) copy-start(bf16[256,12544]{1,0:T(8,128)(2,1)} %param.8) | copy-start | bytes 19267588
  20.0 8.2 %copy-start.5 = (s32[256]{0:T(256)S(1)}, s32[256]{0:T(256)}, u32[]{:S(2)}) copy-start(s32[256]{0:T(256)} %param.11) | copy-start | bytes 3076
  20.0 8.3 %copy-start.4 = (f32[256,128]{1,0:T(8,128)S(1)}, f32[256,128]{1,0:T(8,128)}, u32[]{:S(2)}) copy-start(f32[256,128]{1,0:T(8,128)} %param.9) | copy-start | bytes 393220
  20.0 9.1 %copy-start.7 = (s32[8]{0:T(128)S(1)}, s32[8]{0:T(128)}, u32[]{:S(2)}) copy-start(s32[8]{0:T(128)} %constant.9.clone) | copy-start | bytes 100
  20.1 11.6 %copy-start.6 = (f32[128]{0:T(128)S(1)}, f32[128]{0:T(128)}, u32[]{:S(2)}) copy-start(f32[128]{0:T(128)} %param.12) | copy-start | bytes 1540
  20.1 182.2 %all-to-all-start = ((bf16[8,256,1664]{2,1,0:T(8,128)(2,1)}), bf16[8,256,1664]{2,1,0:T(8,128)(2,1)}, u32[]{:S(2)}, u32[]{:S(2)}) async-start(bf16[8,256,1664]{2,1,0:T(8,128)(2,1)} %bitcast_dynamic-update-slice_fusion), calls=%async_computation | async-start | bytes 13631488 | tf_op jit(solution)/shard_map/all_to_all | solution.py:63
  27.5 148.0 %all-gather.2.cloned.1.call-start = ((), (), s32[]{:S(2)}) async-start(), calls=%async_computation.1 | async-start | bytes 2359296 | tf_op jit(solution)/shard_map/all_gather | solution.py:69
  29.1 315.7 %all-reduce.9.cloned.1.call-start = ((), (), s32[]{:S(2)}) async-start(), calls=%async_computation.2 | async-start | bytes 2105344 | tf_op jit(solution)/shard_map/psum | solution.py:86
  207.6 145.0 %copy-start.3 = (f32[1664,128]{1,0:T(8,128)}, f32[1664,128]{1,0:T(8,128)S(1)}, u32[]{:S(2)}) copy-start(f32[1664,128]{1,0:T(8,128)S(1)} %get-tuple-element.13) | copy-start | bytes 2555908
  215.2 281.2 %all-reduce.11.cloned.1.call-start = ((), (), s32[]{:S(2)}) async-start(), calls=%async_computation.3 | async-start | bytes 2105344 | tf_op jit(solution)/shard_map/psum | solution.py:86
  346.3 5.9 %copy-start = (f32[2056,128]{1,0:T(8,128)S(1)}, f32[2056,128]{1,0:T(8,128)}, u32[]{:S(2)}) copy-start(f32[2056,128]{1,0:T(8,128)} %all-reduce.9.cloned.1.call-done) | copy-start | bytes 3158020
  504.8 6.1 %copy-start.2 = (f32[2056,128]{1,0:T(8,128)S(1)}, f32[2056,128]{1,0:T(8,128)}, u32[]{:S(2)}) copy-start(f32[2056,128]{1,0:T(8,128)} %all-reduce.11.cloned.1.call-done) | copy-start | bytes 3158020
Sparse Core Ops, SparseCore 0:
  31.0 144.4 all-gather.1
  215.3 129.3 all-reduce.8
  365.7 130.7 all-reduce.10
where the time goes:
time: 520 us; the launch traced here: 519 us
  waiting for transfers between devices  418 us (80%)
  matrix products  43.2 us (8%)
  local copies, waits for them, and re-layouts  21.2 us (4%)
  between operations  17.4 us (3%)
  other arithmetic  11.4 us (2%)
  starting transfers between devices  7.75 us (1%)
    psum x2, waiting for transfers between devices, reduced(): total = lax.psum(jnp.concatenate([product, extra]), BOTH)  260 us
    all_gather x1, waiting for transfers between devices, shards(): packed = lax.all_gather(packed, 'tm', axis=0, tiled=True)  140 us
    all_to_all x1, waiting for transfers between devices, shards(): lax.all_to_all(pieces, 'tm', 0, 0).reshape(slabs * epoch_rows, window)  17.8 us
    dot_general x3, matrix products, transposed(): lax.dot_general(columns, filtered, (((0,), (0,)), ((), ())), preferred_el...  15.7 us
    unnamed x26, local copies, waits for them, and re-layouts  12 us
  transfers between devices with their start and end apart: 4, of which 4 were waited for; matrix products, arithmetic and copies ran while one was open for 3% of the time, Pallas kernels for 0%

commit v1 on v0

--- a/solution.py
+++ b/solution.py
@@ -83,7 +83,8 @@
     def reduced(vector, rows):
         product = jnp.dot(columns, vector.astype(jnp.bfloat16), preferred_element_type=jnp.float32)
         extra = jnp.stack(rows + [jnp.zeros_like(rows[0])] * (8 - len(rows)))
-        total = lax.psum(jnp.concatenate([product, extra]), BOTH)
+        xx = jnp.concatenate([product, extra])
+        total = lax.all_gather(xx, axis_name=BOTH).sum(axis=0)
         return (total[: product.shape[0]], [total[product.shape[0] + i] for i in range(len(rows))])
 
     local = jnp.arange(window, dtype=jnp.int32)

time: 520 us -> 668 us (1.28)
  waiting for transfers between devices: 418 us -> 545 us
  other arithmetic: 11.4 us -> 32.6 us
    all_gather x0 -> x2, waiting for transfers between devices: none -> 387 us  [reduced(): total = lax.all_gather(xx, axis_name=BOTH).sum(axis=0)]
    psum x2 -> x0, waiting for transfers between devices: 260 us -> none  [reduced(): total = lax.psum(jnp.concatenate([product, extra]), BOTH)]
    reduce_sum x0 -> x2, other arithmetic: none -> 24.3 us  [reduced(): total = lax.all_gather(xx, axis_name=BOTH).sum(axis=0)]
  transfers between devices with their start and end apart: 4 -> 4, of which waited for: 4 -> 4; matrix products, arithmetic and copies ran while one was open for 3% -> 2% of each run, Pallas kernels for 0% -> 0%
where the time goes in v1:
time: 668 us; the launch traced here: 667 us
  waiting for transfers between devices  545 us (82%)
  matrix products  43.2 us (6%)
  other arithmetic  32.6 us (5%)
  local copies, waits for them, and re-layouts  20.7 us (3%)
  between operations  17.3 us (3%)
  starting transfers between devices  7.75 us (1%)
    all_gather x2, waiting for transfers between devices, reduced(): total = lax.all_gather(xx, axis_name=BOTH).sum(axis=0)  387 us
    all_gather x1, waiting for transfers between devices, shards(): packed = lax.all_gather(packed, 'tm', axis=0, tiled=True)  140 us
    reduce_sum x2, other arithmetic, reduced(): total = lax.all_gather(xx, axis_name=BOTH).sum(axis=0)  24.3 us
    all_to_all x1, waiting for transfers between devices, shards(): lax.all_to_all(pieces, 'tm', 0, 0).reshape(slabs * epoch_rows, window)  17.8 us
    dot_general x3, matrix products, transposed(): lax.dot_general(columns, filtered, (((0,), (0,)), ((), ())), preferred_el...  15.7 us
  transfers between devices with their start and end apart: 4, of which 4 were waited for; matrix products, arithmetic and copies ran while one was open for 2% of the time, Pallas kernels for 0%

profile of v1, /device:TPU:0, one launch (start us, length us, event | category | flops | bytes accessed | tf_op | source)
XLA Modules:
  0.0 666.8 jit_solution(18249154300047697722)
XLA Ops:
  7.2 2.3 bitcast_dynamic-update-slice_fusion.7
  9.5 2.3 bitcast_dynamic-update-slice_fusion.6
  11.7 2.1 bitcast_dynamic-update-slice_fusion.5
  13.8 2.1 bitcast_dynamic-update-slice_fusion.4
  16.0 1.0 bitcast_dynamic-update-slice_fusion.3
  16.9 1.0 bitcast_dynamic-update-slice_fusion.2
  17.9 1.0 bitcast_dynamic-update-slice_fusion.1
  18.9 1.0 bitcast_dynamic-update-slice_fusion
  19.9 7.5 %all-to-all-start = ((bf16[8,256,1664]{2,1,0:T(8,128)(2,1)}), bf16[8,256,1664]{2,1,0:T(8,128)(2,1)}, u32[]{:S(2)}, u32[]{:S(2)}) async-start(bf16[8,256,1664]{2,1,0:T(8,128)(2,1)} %bitcast_dynamic-update-slice_fusion), calls=%async_computation | async-start | bytes 13631488 | tf_op jit(solution)/shard_map/all_to_all | solution.py:63
  28.2 0.7 pad_maximum_fusion
  29.0 0.6 dynamic_slice.15
  31.9 0.3 reshape.60
  32.3 0.3 reshape.59
  33.3 0.8 dynamic-slice_select_fusion.1
  34.1 0.8 dynamic-slice_select_fusion
  34.9 140.5 %all-gather.6.cloned.1.call-done = f32[2048,256]{1,0:T(8,128)} async-done(((f32[256,256]{1,0:T(8,128)}), f32[2048,256]{1,0:T(8,128)}) %all-gather.6.cloned.1.call-update) | async-done | bytes 2097168 | tf_op jit(solution)/shard_map/all_gather | solution.py:69
  175.4 1.6 slice_reduce_fusion
  177.0 1.6 slice_multiply_fusion
  178.6 1.8 fusion.29
  180.4 1.7 fusion.4
  182.1 1.1 fusion.26
  183.2 1.1 fusion.6
  184.3 17.8 %all-to-all-done = bf16[8,256,1664]{2,1,0:T(8,128)(2,1)} async-done(((bf16[8,256,1664]{2,1,0:T(8,128)(2,1)}), bf16[8,256,1664]{2,1,0:T(8,128)(2,1)}, u32[]{:S(2)}, u32[]{:S(2)}) %all-to-all-start) | async-done | bytes 6815776 | tf_op jit(solution)/shard_map/all_to_all | solution.py:63
  202.1 5.3 fusion.15
  207.4 5.3 fusion.20
  212.7 2.2 concatenate.42
  215.2 193.8 %all-gather.8.cloned.1.call-done = f32[65792,128]{1,0:T(8,128)} async-done(((f32[2056,128]{1,0:T(8,128)}), f32[65792,128]{1,0:T(8,128)}) %all-gather.8.cloned.1.call-update) | async-done | bytes 33685520 | tf_op jit(solution)/shard_map/all_gather | solution.py:87
  409.0 12.0 %reduce_sum.87 = f32[2056,128]{1,0:T(8,128)S(1)} reduce(f32[32,2056,128]{2,1,0:T(8,128)} %bitcast.144, f32[]{:T(128)} %constant.4.clone.1), dimensions={0}, to_apply=%region_2.3 | reduce | flops 8158208 | bytes 34738180 | tf_op jit(solution)/shard_map/reduce_sum | solution.py:87
  421.0 0.3 slice_multiply_fusion.1
  421.4 1.8 fusion.28
  423.2 1.7 fusion.3
  424.9 1.1 fusion.25
  426.0 1.1 fusion.10
  427.2 0.4 multiply_reduce_fusion.1
  427.5 5.4 fusion.17
  432.9 5.1 fusion.21
  438.0 2.2 concatenate.45
  440.3 193.1 %all-gather.10.cloned.1.call-done = f32[65792,128]{1,0:T(8,128)} async-done(((f32[2056,128]{1,0:T(8,128)}), f32[65792,128]{1,0:T(8,128)}) %all-gather.10.cloned.1.call-update) | async-done | bytes 33685520 | tf_op jit(solution)/shard_map/all_gather | solution.py:87
  633.5 12.3 %reduce_sum.93 = f32[2056,128]{1,0:T(8,128)S(1)} reduce(f32[32,2056,128]{2,1,0:T(8,128)} %bitcast.143, f32[]{:T(128)} %constant.4.clone.1), dimensions={0}, to_apply=%region_7.8 | reduce | flops 8158208 | bytes 34738180 | tf_op jit(solution)/shard_map/reduce_sum | solution.py:87
  645.8 1.4 multiply_add_fusion
  647.3 0.3 broadcast_multiply_fusion
  647.7 1.8 fusion.27
  649.5 1.7 fusion.2
  651.2 1.1 fusion.24
  652.3 1.2 fusion.9
  653.5 0.4 multiply_reduce_fusion
  653.9 4.9 fusion.37
  658.8 1.4 dynamic-slice_subtract_fusion
  (37 shorter events, 1.2 us)
Async XLA Ops:
  7.2 8.8 %copy-start = (bf16[256,12544]{1,0:T(8,128)(2,1)S(1)}, bf16[256,12544]{1,0:T(8,128)(2,1)}, u32[]{:S(2)}) copy-start(bf16[256,12544]{1,0:T(8,128)(2,1)} %param.8) | copy-start | bytes 19267588
  19.9 8.2 %copy-start.3 = (s32[256]{0:T(256)S(1)}, s32[256]{0:T(256)}, u32[]{:S(2)}) copy-start(s32[256]{0:T(256)} %param.11) | copy-start | bytes 3076
  19.9 8.3 %copy-start.2 = (f32[256,128]{1,0:T(8,128)S(1)}, f32[256,128]{1,0:T(8,128)}, u32[]{:S(2)}) copy-start(f32[256,128]{1,0:T(8,128)} %param.9) | copy-start | bytes 393220
  19.9 9.1 %copy-start.5 = (s32[8]{0:T(128)S(1)}, s32[8]{0:T(128)}, u32[]{:S(2)}) copy-start(s32[8]{0:T(128)} %constant.9.clone) | copy-start | bytes 100
  19.9 11.6 %copy-start.4 = (f32[128]{0:T(128)S(1)}, f32[128]{0:T(128)}, u32[]{:S(2)}) copy-start(f32[128]{0:T(128)} %param.12) | copy-start | bytes 1540
  19.9 182.2 %all-to-all-start = ((bf16[8,256,1664]{2,1,0:T(8,128)(2,1)}), bf16[8,256,1664]{2,1,0:T(8,128)(2,1)}, u32[]{:S(2)}, u32[]{:S(2)}) async-start(bf16[8,256,1664]{2,1,0:T(8,128)(2,1)} %bitcast_dynamic-update-slice_fusion), calls=%async_computation | async-start | bytes 13631488 | tf_op jit(solution)/shard_map/all_to_all | solution.py:63
  27.4 148.0 %all-gather.6.cloned.1.call-start = ((), (), s32[]{:S(2)}) async-start(), calls=%async_computation.1 | async-start | bytes 2359296 | tf_op jit(solution)/shard_map/all_gather | solution.py:69
  28.9 380.1 %all-gather.8.cloned.1.call-start = ((), (), s32[]{:S(2)}) async-start(), calls=%async_computation.2 | async-start | bytes 34738176 | tf_op jit(solution)/shard_map/all_gather | solution.py:87
  207.4 220.1 %copy-start.1 = (f32[1664,128]{1,0:T(8,128)}, f32[1664,128]{1,0:T(8,128)S(1)}, u32[]{:S(2)}) copy-start(f32[1664,128]{1,0:T(8,128)S(1)} %get-tuple-element.13) | copy-start | bytes 2555908
  215.0 418.5 %all-gather.10.cloned.1.call-start = ((), (), s32[]{:S(2)}) async-start(), calls=%async_computation.3 | async-start | bytes 34738176 | tf_op jit(solution)/shard_map/all_gather | solution.py:87
Sparse Core Ops, SparseCore 0:
  30.9 144.4 all-gather.5
  215.1 193.8 all-gather.7
  440.4 193.0 all-gather.9
